TPU v7x, 128 devices: a whole 4x4x4 slice. The times are simulated.
128 devices in a mesh: tm: 2 (over core), stn: 8 (over y_hi, z), chan: 8 (over x, y_lo).
Axes of the slice: x: 4, y: 4 (y_hi: 2, y_lo: 2; y = y_hi * 2 + y_lo), z: 4, core: 2. Of those that a mesh axis runs over, the one named last changes fastest.
Arguments:
- voltages: bfloat16 [2, 8, 512, 32, 2, 256], P(None, 'chan', 'stn', 'tm'), may hold values from -100 to 100
- fir_taps: float32 [16, 256], replicated, may hold values from -1.5 to 1.5
- station_map: int32 [512], P('stn'), may hold values from 0 to 31, as said below
- beam_index: int32 [512], P('stn'), may hold values from 0 to 15
- weight_table: bfloat16 [2, 16, 8, 8], P(None, None, 'chan'), may hold values from -1.5 to 1.5
Outputs:
- visibilities: float32 [2, 2, 8, 32, 32, 8, 2, 2, 256], P('tm', None, 'chan', 'stn')
Inputs may be any that keep to these rules, and one draw needn't show every extreme that they name: `station_map`: each station number names exactly 16 dishes; of the dishes g * 64 up to (g + 1) * 64 - 1, exactly 8 name a station of the block h * 4 up to (h + 1) * 4 - 1, for every g and h.
All inputs are finite; a program needn't handle non-finite values.
Results may differ from a plain program's by a relative error of at most 0.017.
Values may be sent and summed in bfloat16 or wider, within the bound.
A program may use at most 512 MiB of HBM per device.

v0:
```python
import jax
import jax.numpy as jnp
from jax import lax
from jax.sharding import PartitionSpec as P

STATIONS = 32
COARSE = 8


epsilon = 1e-06


def shifted(value, axis, steps):
    count = lax.axis_size(axis)
    first, last = (max(0, -steps), min(count, count - steps))
    return lax.ppermute(value, axis, [(source, source + steps) for source in range(first, last)])


def rows_first(arrays, axis, dims):
    turned = [jnp.moveaxis(a, dim, 0) for a, dim in zip(arrays, dims)]
    widths = [t[0].size for t in turned]
    both = jnp.concatenate([t.reshape(-1, w) for t, w in zip(turned, widths)], axis=1)
    whole = lax.all_gather(both, axis, axis=0, tiled=True)
    pieces = jnp.split(whole, [sum(widths[:k]) for k in range(1, len(widths))], axis=1)
    return tuple(
        (
            jnp.moveaxis(b.reshape(-1, *t.shape[1:]), 0, dim)
            for b, t, dim in zip(pieces, turned, dims)
        )
    )


def split_up(shard, dim, count):
    shape = shard.shape
    pieces = shard.reshape(*shape[:dim], count, shape[dim] // count, *shape[dim + 1 :])
    return jnp.moveaxis(pieces, dim, 0)


def cut_rows(length, count):
    hop = length // count
    if hop >= 8:
        hop -= hop % 8
    return [hop * k for k in range(1, count)]


def in_order(pieces, dim):
    shape = list(pieces.shape[1:])
    shape[dim] *= pieces.shape[0]
    return jnp.moveaxis(pieces, 0, dim).reshape(shape)


def several_exchanges(shard, axis, pieces, split_dim, concat_dim):
    blocks = split_up(shard, split_dim, lax.axis_size(axis))
    widest = max(range(1, max(2, blocks.ndim - 1)), key=lambda d: blocks.shape[d])
    outs = []
    for section in jnp.split(blocks, cut_rows(blocks.shape[widest], pieces), axis=widest):
        if section.size:
            outs.append(lax.all_to_all(section, axis, split_axis=0, concat_axis=0, tiled=True))
    return in_order(jnp.concatenate(outs, axis=widest), concat_dim)


def from_everyone(shard, axis):
    count = lax.axis_size(axis)
    return lax.all_to_all(
        jnp.broadcast_to(shard[None], (count, *shard.shape)), axis, 0, 0, tiled=True
    )


def taken_together(shard, axis):
    return from_everyone(shard, axis).sum(axis=0)


def dft_tables(length):
    bin_index = jnp.arange(length, dtype=jnp.int32)
    phase_step = bin_index[:, None] * bin_index[None, :] % length
    angles = phase_step.astype(jnp.float32) * (2.0 * jnp.pi / length)
    return (jnp.cos(angles).astype(jnp.bfloat16), jnp.sin(angles).astype(jnp.bfloat16))


def power_terms(formed):
    values = formed.astype(jnp.float32)
    return jnp.sum(values * values, axis=(1, 3, 4, 6))


def normalise(formed, power_sum, denominator):
    inverse_rms = lax.rsqrt(power_sum / denominator + epsilon)
    return (formed.astype(jnp.float32) * inverse_rms[:, None, :, None, None, :, None]).astype(
        jnp.bfloat16
    )


def correlate(left_beams, right_beams, frames_dev):

    def product(first_part, second_part):
        return jnp.einsum(
            "sbcfpk,tbcfqk->cstbpqk", first_part, second_part, preferred_element_type=jnp.float32
        )

    left_re = left_beams[:, 0]
    left_im = left_beams[:, 1]
    right_re = right_beams[:, 0]
    right_im = right_beams[:, 1]
    vis_re = product(left_re, right_re) + product(left_im, right_im)
    vis_im = product(left_im, right_re) - product(left_re, right_im)
    return jnp.stack([vis_re, vis_im]) / frames_dev


def mixing_of(row_hot, weight_table):
    weights = jnp.einsum("dt,otcb->ocdb", row_hot, weight_table, preferred_element_type=jnp.float32)
    weight_re = weights[0]
    weight_im = weights[1]
    return jnp.stack([jnp.stack([weight_re, -weight_im]), jnp.stack([weight_im, weight_re])])


def per_device(voltages, fir_taps, station_map, beam_index, weight_table):
    components, coarse_dev, dishes_dev, frames_dev, polars, fine_bins = voltages.shape
    history = fir_taps.shape[0] - 1
    table_rows = weight_table.shape[1]
    cosine, sine_table = dft_tables(fine_bins)
    earlier = shifted(voltages[:, :, :, frames_dev - history :], "tm", 1)
    extended = jnp.concatenate([earlier, voltages], axis=3)
    filtered = jnp.zeros(voltages.shape, jnp.float32)
    for tap_index in range(history + 1):
        offset = history - tap_index
        filtered = filtered + fir_taps[tap_index] * extended[
            :, :, :, offset : offset + frames_dev
        ].astype(jnp.float32)
    filtered = filtered.astype(jnp.bfloat16)
    real_part = filtered[0].reshape(-1, fine_bins)
    imag_part = filtered[1].reshape(-1, fine_bins)
    spec_re = jnp.dot(real_part, cosine, preferred_element_type=jnp.float32) + jnp.dot(
        imag_part, sine_table, preferred_element_type=jnp.float32
    )
    spec_im = jnp.dot(imag_part, cosine, preferred_element_type=jnp.float32) - jnp.dot(
        real_part, sine_table, preferred_element_type=jnp.float32
    )
    spectra = jnp.stack([spec_re, spec_im]).reshape(voltages.shape).astype(jnp.bfloat16)
    denominator = COARSE * frames_dev * fine_bins
    own_count = STATIONS // lax.axis_size("stn")
    stn_count = lax.axis_size("stn")
    full_map, full_rows = rows_first((station_map, beam_index), "stn", (0, 0))
    share = dishes_dev // stn_count
    target = station_map // own_count
    target_hot = (target[:, None] == jnp.arange(stn_count, dtype=jnp.int32)[None, :]).astype(
        jnp.int32
    )
    rank = jnp.sum((jnp.cumsum(target_hot, axis=0) - 1) * target_hot, axis=1)
    slot = target * share + rank
    reorder = (slot[None, :] == jnp.arange(dishes_dev, dtype=jnp.int32)[:, None]).astype(
        jnp.bfloat16
    )
    ordered = jnp.einsum(
        "ed,ocdfpk->ocefpk", reorder, spectra, preferred_element_type=jnp.float32
    ).astype(jnp.bfloat16)
    arrived = several_exchanges(ordered, "stn", 2, 2, 2)
    holder = lax.axis_index("stn")
    owner_mask = (full_map // own_count == holder).astype(jnp.int32)
    position = jnp.cumsum(owner_mask) - 1
    pick = owner_mask[:, None] * (
        position[:, None] == jnp.arange(dishes_dev, dtype=jnp.int32)[None, :]
    ).astype(jnp.int32)
    local_station = jnp.sum(pick * (full_map - holder * own_count)[:, None], axis=0)
    local_row = jnp.sum(pick * full_rows[:, None], axis=0)
    station_own = (
        local_station[:, None] == jnp.arange(own_count, dtype=jnp.int32)[None, :]
    ).astype(jnp.float32)
    row_hot = (local_row[:, None] == jnp.arange(table_rows, dtype=jnp.int32)[None, :]).astype(
        jnp.bfloat16
    )
    mixing = mixing_of(row_hot, weight_table)
    beams = mixing.shape[-1]
    steer_own = (station_own[None, None, None, :, :, None] * mixing[:, :, :, :, None, :]).astype(
        jnp.bfloat16
    )
    steer_groups = steer_own.reshape(2, 2, coarse_dev, stn_count, share, own_count, beams)
    spec_groups = arrived.reshape(2, coarse_dev, stn_count, share, frames_dev, polars, fine_bins)
    partials = jnp.einsum(
        "oicgdsb,icgdfpk->gsobcfpk", steer_groups, spec_groups, preferred_element_type=jnp.float32
    ).astype(jnp.bfloat16)
    formed = jnp.sum(partials.astype(jnp.float32), axis=0).astype(jnp.bfloat16)
    power_sum = taken_together(power_terms(formed), "chan")
    normed = normalise(formed, power_sum, denominator)
    visibility = correlate(normed, lax.all_gather(normed, "stn", axis=0, tiled=True), frames_dev)
    return visibility[None]


def solution(mesh):
    in_specs = (
        P(None, "chan", "stn", "tm", None, None),
        P(),
        P("stn"),
        P("stn"),
        P(None, None, "chan", None),
    )
    out_specs = P("tm", None, "chan", "stn", None, None, None, None, None)
    return jax.shard_map(
        per_device, mesh=mesh, in_specs=in_specs, out_specs=out_specs, check_vma=False
    )
```

profile of v0, /device:TPU:1, one launch (start us, length us, event | category | flops | bytes accessed | tf_op | source)
XLA Modules:
  0.0 418.3 jit_solution(10136735637270624918)
XLA Ops:
  6.5 4.3 %slice.129 = bf16[2,1,64,15,2,256]{5,4,3,2,1,0:T(2,128)(2,1)} slice(bf16[2,1,64,16,2,256]{5,4,3,2,1,0:T(2,128)(2,1)} %param.5), slice={[0:2], [0:1], [0:64], [1:16], [0:2], [0:256]} | slice | bytes 3932160 | tf_op jit(solution)/shard_map/slice | solution.py:120
  10.9 1.3 collective-permute-start
  12.1 0.7 and_select_fusion.1
  12.8 0.1 fusion.40
  12.9 0.1 reduce_window_sum.28
  13.0 0.2 select_reduce_fusion
  13.2 0.7 multiply_add_fusion
  13.8 1.0 fusion.72
  14.9 2.4 collective-permute-done
  17.3 2.9 constant_dynamic-update-slice_fusion.1
  20.2 2.2 constant_dynamic-update-slice_fusion
  22.4 27.4 %add_convert_fusion = bf16[2,1,64,16,2,256]{5,4,3,2,1,0:T(2,128)(2,1)S(1)} fusion(bf16[2,1,64,16,2,256]{5,4,3,2,1,0:T(2,128)(2,1)S(1)} %copy-done.2, bf16[2,1,64,31,2,256]{5,4,3,2,1,0:T(2,128)(2,1)S(1)} %constant_dynamic-update-slice_fusion, f32[256]{0:T(256)S(1)} %bitcast.169, f32[256]{0:T(256)S(1)} %bitcast.170, f32[256]{0:T(256)S(1)} %bitcast.156, ...), kind=kLoop, calls=%fused_computation.12 | loop fusion | flops 50331648 | bytes 35667968 | tf_op jit(solution)/shard_map/convert_element_type | solution.py:128
  49.9 1.8 fusion.71
  51.7 0.4 reshape_squeeze.6
  52.2 2.7 fusion.39
  54.9 0.4 reshape_squeeze.7
  55.3 2.7 fusion.38
  58.0 2.4 fusion.12
  60.4 2.4 stack.34
  62.8 2.8 copy.74
  65.7 2.4 fusion.13
  68.0 1.6 stack.35
  69.6 0.6 copy.75
  70.2 0.7 convert_bitcast_fusion.1
  70.9 0.3 copy.115
  71.2 1.5 fusion.70
  72.8 8.2 %all-to-all-start = ((bf16[8,2,1,8,8,2,256]{6,3,1,5,4,2,0:T(8,128)(2,1)}), bf16[8,2,1,8,8,2,256]{6,3,1,5,4,2,0:T(8,128)(2,1)S(1)}, u32[]{:S(2)}, u32[]{:S(2)}) async-start(bf16[8,2,1,8,8,2,256]{6,3,1,5,4,2,0:T(8,128)(2,1)} %get-tuple-element.9), calls=%async_computation | async-start | bytes 2097152 | tf_op jit(solution)/shard_map/all_to_all | solution.py:58
  81.0 25.7 %all-gather = s32[8,64,2]{1,2,0:T(2,128)S(1)} all-gather(s32[1,64,2]{1,2,0:T(2,128)S(1)} %add_bitcast_fusion.2), channel_id=1, replica_groups=mesh['tm'=2,'stn'=8,'chan'=8] {'stn'}, dimensions={0}, use_global_device_ids=true | all-gather | bytes 4608 | tf_op jit(solution)/shard_map/all_gather | solution.py:23
  106.7 0.1 reshape.281
  106.8 0.3 reduce-window.9
  107.1 0.1 slice.161
  107.2 0.1 slice_reduce_fusion
  107.4 3.6 all-to-all-start.1
  111.0 0.0 all-gather.3.cloned.1.call-start
  111.0 0.1 add_bitcast_fusion.1
  111.1 0.1 fusion.36
  111.2 0.1 convolution_bitcast_fusion
  111.4 0.1 stack.38
  111.5 0.1 stack.40
  111.6 0.1 eq.98
  111.7 10.3 %all-to-all-done.1 = bf16[8,2,1,8,8,2,256]{6,3,1,5,4,2,0:T(8,128)(2,1)S(1)} async-done(((bf16[8,2,1,8,8,2,256]{6,3,1,5,4,2,0:T(8,128)(2,1)}), bf16[8,2,1,8,8,2,256]{6,3,1,5,4,2,0:T(8,128)(2,1)S(1)}, u32[]{:S(2)}, u32[]{:S(2)}) %all-to-all-start.1) | async-done | bytes 1048608 | tf_op jit(solution)/shard_map/all_to_all | solution.py:58
  121.9 2.8 fusion.14
  124.8 0.3 fusion.17
  125.1 0.1 copy.111
  125.2 0.1 copy.82
  125.3 9.1 %all_to_all.15 = f32[8,4,8,2]{2,1,3,0:T(4,128)S(1)} all-to-all(f32[8,4,8,2]{2,1,3,0:T(4,128)S(1)} %broadcast_in_dim.2), channel_id=1, replica_groups=mesh['tm'=2,'stn'=8,'chan'=8] {'chan'}, dimensions={0} | all-to-all | bytes 4096 | tf_op jit(solution)/shard_map/all_to_all | solution.py:64
  134.5 0.6 fusion.16
  135.0 1.7 copy.83
  136.7 0.0 all-gather.3.cloned.1.call-update
  136.7 0.1 slice_bitcast_fusion
  136.8 3.6 copy.100
  140.4 3.5 copy.98
  143.9 102.6 %all-gather.3.cloned.1.call-done = bf16[32,2,8,1,16,2,256]{6,4,5,3,2,1,0:T(8,128)(2,1)} async-done(((bf16[4,2,8,1,16,2,256]{6,4,5,3,2,1,0:T(8,128)(2,1)}), bf16[32,2,8,1,16,2,256]{6,4,5,3,2,1,0:T(8,128)(2,1)}) %all-gather.3.cloned.1.call-update) | async-done | bytes 8388624 | tf_op jit(solution)/shard_map/all_gather | solution.py:183
  246.4 6.3 %fusion.69 = (bf16[32,1,8,1,16,2,256]{6,4,5,3,2,1,0:T(8,128)(2,1)}, bf16[32,1,8,1,16,2,256]{6,4,5,3,2,1,0:T(8,128)(2,1)}) fusion(bf16[32,2,8,1,16,2,256]{6,4,5,3,2,1,0:T(8,128)(2,1)} %all-gather.3.cloned.1.call-done), kind=kLoop, calls=%fused_computation.116 | loop fusion | bytes 16777216 | tf_op jit(solution)/shard_map/slice | solution.py:101
  252.7 28.5 %copy.113 = bf16[32,1,8,1,16,2,256]{0,4,5,6,2,3,1:T(8,128)(2,1)} copy(bf16[32,1,8,1,16,2,256]{6,4,5,3,2,1,0:T(8,128)(2,1)} %get-tuple-element.8) | data formatting | bytes 8388608
  281.2 28.5 %copy.112 = bf16[32,1,8,1,16,2,256]{0,4,5,6,2,3,1:T(8,128)(2,1)} copy(bf16[32,1,8,1,16,2,256]{6,4,5,3,2,1,0:T(8,128)(2,1)} %get-tuple-element.7) | data formatting | bytes 8388608
  309.7 15.5 %fusion.2 = f32[8,256,32,2,4,2]{2,4,5,3,1,0:T(4,128)} fusion(bf16[4,8,16,2,256,1]{2,0,3,5,4,1:T(4,128)(2,1)} %copy.100, bf16[32,1,8,1,16,2,256]{0,4,5,6,2,3,1:T(8,128)(2,1)} %copy.113), kind=kOutput, calls=%fused_computation.2 | convolution fusion | flops 33554432 | bytes 8912896 | tf_op jit(solution)/shard_map/sbcfpk,tbcfqk->cstbpqk/dot_general | solution.py:95
  325.2 15.5 %fusion = f32[8,256,32,2,4,2]{2,4,5,3,1,0:T(4,128)} fusion(bf16[4,8,16,2,256,1]{2,0,3,5,4,1:T(4,128)(2,1)} %copy.98, bf16[32,1,8,1,16,2,256]{0,4,5,6,2,3,1:T(8,128)(2,1)} %copy.113), kind=kOutput, calls=%fused_computation | convolution fusion | flops 33554432 | bytes 8912896 | tf_op jit(solution)/shard_map/sbcfpk,tbcfqk->cstbpqk/dot_general | solution.py:95
  340.7 18.2 %add_bitcast_fusion = f32[1,1,1,4,32,8,2,2,256]{4,3,6,7,8,5,2,1,0:T(4,128)} fusion(f32[8,256,32,2,4,2]{2,4,5,3,1,0:T(4,128)} %fusion.2, bf16[4,8,16,2,256,1]{2,0,3,5,4,1:T(4,128)(2,1)} %copy.98, bf16[32,1,8,1,16,2,256]{0,4,5,6,2,3,1:T(8,128)(2,1)} %copy.112), kind=kOutput, calls=%fused_computation.10 | convolution fusion | flops 34603008 | bytes 13107200 | tf_op jit(solution)/shard_map/sbcfpk,tbcfqk->cstbpqk/dot_general | solution.py:95
  358.9 11.6 %copy.90 = f32[1,1,1,4,32,8,2,2,256]{8,5,7,6,4,3,2,1,0:T(8,128)} copy(f32[1,1,1,4,32,8,2,2,256]{4,3,6,7,8,5,2,1,0:T(4,128)} %add_bitcast_fusion) | data formatting | bytes 8388608 | tf_op jit(solution)/shard_map/stack | solution.py:105
  370.5 18.3 %subtract_bitcast_fusion = f32[1,1,1,4,32,8,2,2,256]{4,3,6,7,8,5,2,1,0:T(4,128)} fusion(f32[8,256,32,2,4,2]{2,4,5,3,1,0:T(4,128)} %fusion, bf16[4,8,16,2,256,1]{2,0,3,5,4,1:T(4,128)(2,1)} %copy.100, bf16[32,1,8,1,16,2,256]{0,4,5,6,2,3,1:T(8,128)(2,1)} %copy.112), kind=kOutput, calls=%fused_computation.9 | convolution fusion | flops 34603008 | bytes 13107200 | tf_op jit(solution)/shard_map/sbcfpk,tbcfqk->cstbpqk/dot_general | solution.py:95
  388.8 11.5 %copy.91 = f32[1,1,1,4,32,8,2,2,256]{8,5,7,6,4,3,2,1,0:T(8,128)} copy(f32[1,1,1,4,32,8,2,2,256]{4,3,6,7,8,5,2,1,0:T(4,128)} %subtract_bitcast_fusion) | data formatting | bytes 8388608 | tf_op jit(solution)/shard_map/stack | solution.py:105
  400.3 4.5 %maximum_multiply_fusion = f32[1,2,1,4,32,8,2,2,256]{8,5,7,6,4,3,2,1,0:T(8,128)S(1)} fusion(f32[1,1,1,4,32,8,2,2,256]{8,5,7,6,4,3,2,1,0:T(8,128)} %copy.91, f32[1,1,1,4,32,8,2,2,256]{8,5,7,6,4,3,2,1,0:T(8,128)} %copy.90), kind=kLoop, calls=%fused_computation.11 | loop fusion | flops 4194304 | bytes 16777216 | tf_op jit(solution)/shard_map/div | solution.py:105
  404.9 6.6 %copy.92 = f32[1,2,1,4,32,8,2,2,256]{8,7,6,5,4,3,2,1,0:T(2,128)} copy(f32[1,2,1,4,32,8,2,2,256]{8,5,7,6,4,3,2,1,0:T(8,128)S(1)} %maximum_multiply_fusion) | data formatting | bytes 16777216 | tf_op jit(solution)/shard_map/div | solution.py:105
  (31 shorter events, 0.2 us)
Async XLA Ops:
  6.5 104.7 %copy-start = (bf16[2,16,1,8]{1,3,2,0:T(8,128)(2,1)S(1)}, bf16[2,16,1,8]{1,3,2,0:T(8,128)(2,1)}, u32[]{:S(2)}) copy-start(bf16[2,16,1,8]{1,3,2,0:T(8,128)(2,1)} %param.9) | copy-start | bytes 1540
  6.5 13.7 %copy-start.2 = (bf16[2,1,64,16,2,256]{5,4,3,2,1,0:T(2,128)(2,1)S(1)}, bf16[2,1,64,16,2,256]{5,4,3,2,1,0:T(2,128)(2,1)}, u32[]{:S(2)}) copy-start(bf16[2,1,64,16,2,256]{5,4,3,2,1,0:T(2,128)(2,1)} %param.5) | copy-start | bytes 6291460
  10.9 6.5 %collective-permute-start = (bf16[2,1,64,15,2,256]{5,4,3,2,1,0:T(2,128)(2,1)}, bf16[2,1,64,15,2,256]{5,4,3,2,1,0:T(2,128)(2,1)}, u32[]{:S(2)}, u32[]{:S(2)}) collective-permute-start(bf16[2,1,64,15,2,256]{5,4,3,2,1,0:T(2,128)(2,1)} %slice.129), channel_id=1, source_target_pairs={{0,64},{1,65},{2,66},{3,67},{4,68},{5,69},{6,70},{7,71},{8,72},{9,... | collective-permute-start | bytes 5898248 | tf_op jit(solution)/shard_map/ppermute | solution.py:16
  55.3 2.7 copy-start.4
  60.4 5.3 %copy-start.3 = (f32[2048,256]{1,0:T(8,128)S(1)}, f32[2048,256]{1,0:T(8,128)}, u32[]{:S(2)}) copy-start(f32[2048,256]{1,0:T(8,128)} %fusion.38) | copy-start | bytes 6291460
  68.0 2.2 copy-start.5
  71.2 9.8 %copy-start.6 = (s32[64]{0:T(128)S(1)}, s32[64]{0:T(128)}, u32[]{:S(2)}) copy-start(s32[64]{0:T(128)} %param.7) | copy-start | bytes 772
  71.2 9.8 %copy-start.7 = (s32[64]{0:T(128)S(1)}, s32[64]{0:T(128)}, u32[]{:S(2)}) copy-start(s32[64]{0:T(128)} %param.8) | copy-start | bytes 772
  72.8 34.6 %all-to-all-start = ((bf16[8,2,1,8,8,2,256]{6,3,1,5,4,2,0:T(8,128)(2,1)}), bf16[8,2,1,8,8,2,256]{6,3,1,5,4,2,0:T(8,128)(2,1)S(1)}, u32[]{:S(2)}, u32[]{:S(2)}) async-start(bf16[8,2,1,8,8,2,256]{6,3,1,5,4,2,0:T(8,128)(2,1)} %get-tuple-element.9), calls=%async_computation | async-start | bytes 2097152 | tf_op jit(solution)/shard_map/all_to_all | solution.py:58
  107.4 14.6 %all-to-all-start.1 = ((bf16[8,2,1,8,8,2,256]{6,3,1,5,4,2,0:T(8,128)(2,1)}), bf16[8,2,1,8,8,2,256]{6,3,1,5,4,2,0:T(8,128)(2,1)S(1)}, u32[]{:S(2)}, u32[]{:S(2)}) async-start(bf16[8,2,1,8,8,2,256]{6,3,1,5,4,2,0:T(8,128)(2,1)} %get-tuple-element.10), calls=%async_computation.1 | async-start | bytes 2097152 | tf_op jit(solution)/shard_map/all_to_all | solution.py:58
  111.0 135.5 %all-gather.3.cloned.1.call-start = ((), (), s32[]{:S(2)}) async-start(), calls=%async_computation.3 | async-start | bytes 9437184 | tf_op jit(solution)/shard_map/all_gather | solution.py:183
  404.9 6.6 %copy-start.1 = (bf16[2,16,1,8]{1,3,2,0:T(8,128)(2,1)S(1)}, bf16[2,16,1,8]{1,3,2,0:T(8,128)(2,1)}, u32[]{:S(2)}) copy-start(bf16[2,16,1,8]{1,3,2,0:T(8,128)(2,1)} %param.9) | copy-start | bytes 1540
Sparse Core Ops, SparseCore 0:
  136.8 109.5 all-gather.2
where the time goes:
time: 419 us; the launch traced here: 418 us
  local copies, waits for them, and re-layouts  125 us (30%)
  waiting for transfers between devices  115 us (27%)
  matrix products  81.3 us (19%)
  other arithmetic  35.2 us (8%)
  blocking collectives  34.8 us (8%)
  between operations  13.7 us (3%)
  starting transfers between devices  13.1 us (3%)
    all_gather x1, waiting for transfers between devices, per_device(): lax.all_gather(normed, 'stn', axis=0, tiled=True)  103 us
    dot_general x4, matrix products, product(): jnp.einsum('sbcfpk,tbcfqk->cstbpqk', first_part, second_part, preferred_e...  67.4 us
    unnamed x21, local copies, waits for them, and re-layouts  60.1 us
    convert_element_type x1, other arithmetic, per_device(): filtered = filtered.astype(jnp.bfloat16)  27.4 us
    all_gather x1, blocking collectives, rows_first(): whole = lax.all_gather(both, axis, axis=0, tiled=True)  25.7 us
    another operation x2, local copies, waits for them, and re-layouts, correlate(): return jnp.stack([vis_re, vis_im]) / frames_dev  23.1 us
    all_to_all x2, starting transfers between devices, several_exchanges(): lax.all_to_all(section, axis, split_axis=0, concat_axis=0, tiled=True)  11.8 us
    all_to_all x2, waiting for transfers between devices, several_exchanges(): lax.all_to_all(section, axis, split_axis=0, concat_axis=0, tiled=True)  10.3 us
  transfers between devices with their start and end apart: 4, of which 3 were waited for; matrix products, arithmetic and copies ran while one was open for 3% of the time, Pallas kernels for 0%

commit v1 on v0

v1 whole, which is shorter than its diff:
```python
import functools

import jax
import jax.numpy as jnp
import numpy as np
from jax import lax
from jax.experimental import pallas as pl
from jax.experimental.pallas import tpu as pltpu
from jax.sharding import PartitionSpec as P

MESH = pl.DeviceIdType.MESH
F32 = jnp.float32
BF16 = jnp.bfloat16
EPSILON = 1e-06
STN = 8
RING = 4
CHAN = 8
SHARE = 8
OWN = 4
BEAMS = 8
POL = 2
FRAMES = 16
TAPS = 16
FINE = 256
LANES = 128
NT = FINE // LANES
HISTORY = TAPS - 1
PITCH = 72
DENOMINATOR = float(CHAN * FRAMES * FINE)


def dft_table():
    step = np.arange(FINE)
    angle = (step[:, None] * step[None, :] % FINE) * (2.0 * np.pi / FINE)
    cosine, sine = np.cos(angle), np.sin(angle)
    return np.block([[cosine, -sine], [sine, cosine]]).astype(np.float32)


def kernel(
    perm_ref, v_ref, wt_ref, taps_ref, tab_ref, out_ref,
    regroup, send_v, recv_v, recv_wt, weights, beams, filtered, formed, scaled, stage, packed,
    power, power_all, inverse,
    a_send, a_recv, w_send, w_recv, h_send, h_recv, g_send, g_recv, f_send,
    p_send, p_recv, i_send, i_recv, o_sem, x_send, x_recv,
):
    half = lax.axis_index("tm")
    me = lax.axis_index("stn")
    chan = lax.axis_index("chan")
    row, col = me // RING, me % RING
    up = row * RING + lax.rem(col + 1, RING)
    down = row * RING + lax.rem(col + 3, RING)
    far = row * RING + lax.rem(col + 2, RING)
    pair = (1 - row) * RING + col
    peers = {1: up, 2: far, 3: down, 4: pair}

    def remote(src, dst, send, recv, **where):
        return pltpu.make_async_remote_copy(
            src_ref=src, dst_ref=dst, send_sem=send, recv_sem=recv,
            device_id=where, device_id_type=MESH,
        )

    barrier = pltpu.get_barrier_semaphore()
    pl.semaphore_signal(barrier, inc=1, device_id={"tm": 1 - half}, device_id_type=MESH)
    for step in range(1, STN):
        pl.semaphore_signal(
            barrier, inc=1, device_id={"stn": lax.rem(me + step, STN)}, device_id_type=MESH
        )
    for step in range(1, CHAN):
        pl.semaphore_signal(
            barrier, inc=1, device_id={"chan": lax.rem(chan + step, CHAN)}, device_id_type=MESH
        )

    def regrouped(step, store):
        holder = lax.rem(me + step, STN)
        for part in range(2):
            for e in range(SHARE):
                dish = perm_ref[holder * SHARE + e]
                line = (part * SHARE + e) * PITCH
                regroup[line : line + FRAMES * NT * POL, :] = v_ref[part, dish].astype(F32)
        for pol in range(POL):
            for tile in range(FRAMES * NT):
                value = regroup[pl.ds(tile * POL + pol, 2 * SHARE, stride=PITCH), :]
                store(pol, tile * LANES, value.astype(BF16))

    mine = pl.ds(pl.multiple_of(me * 2 * SHARE, 2 * SHARE), 2 * SHARE)

    def dish_copy(pol, step):
        return remote(
            send_v.at[step - 1, pol], recv_v.at[pol, mine],
            a_send.at[pol, step - 1], a_recv.at[pol, step - 1], stn=lax.rem(me + step, STN),
        )

    def weight_copy(step):
        holder = lax.rem(me + step, STN)
        return remote(
            wt_ref.at[holder], recv_wt.at[mine], w_send.at[step - 1], w_recv.at[step - 1], stn=holder
        )

    def prepare(step, carry):
        def store(pol, lane, value):
            send_v[step - 1, pol, :, lane : lane + LANES] = value

        regrouped(step, store)
        return carry

    def prepare_and_send(step, carry):
        prepare(step, carry)
        dish_copy(0, step - 1).start()
        return carry

    prepare(1, 0)
    pl.semaphore_wait(barrier, 1 + (STN - 1) + (CHAN - 1))
    for step in range(1, STN):
        weight_copy(step).start()
    lax.fori_loop(2, STN, prepare_and_send, 0)

    def store_own(pol, lane, value):
        recv_v[pol, mine, lane : lane + LANES] = value

    regrouped(0, store_own)
    dish_copy(0, STN - 1).start()
    lax.fori_loop(1, STN, lambda step, c: (dish_copy(1, step).start(), c)[1], 0)
    recv_wt[mine, :] = wt_ref[me]
    power[...] = jnp.zeros_like(power)
    lane_id = lax.broadcasted_iota(jnp.int32, (BEAMS, LANES), 1)

    for step in range(1, STN):
        weight_copy(step).wait_recv()
    weights[...] = jnp.transpose(recv_wt[...].astype(F32))[: 2 * OWN * BEAMS, :].astype(BF16)

    def halo_copy(pol):
        return remote(
            beams.at[pol, :, pl.ds((HISTORY + 1) * BEAMS, HISTORY * BEAMS), :],
            beams.at[pol, :, pl.ds(0, HISTORY * BEAMS), :],
            h_send.at[pol], h_recv.at[pol], tm=1 - half,
        )

    def chunk_copies(chunk):
        own = formed.at[0, chunk]
        return (
            remote(own, formed.at[3, chunk], g_send.at[0, chunk], g_recv.at[3, chunk], stn=up),
            remote(own, formed.at[1, chunk], g_send.at[1, chunk], g_recv.at[1, chunk], stn=down),
            remote(own, formed.at[4, chunk], g_send.at[2, chunk], g_recv.at[4, chunk], stn=pair),
        )

    for pol in range(POL):
        lax.fori_loop(1, STN, lambda step, c: (dish_copy(pol, step).wait_recv(), c)[1], 0)

        def steer(frame, carry):
            lanes = pl.ds(pl.multiple_of(frame * FINE, FINE), FINE)
            value = jnp.dot(weights[...], recv_v[pol, :, lanes], preferred_element_type=F32)
            line = pl.ds(pl.multiple_of((HISTORY + frame) * BEAMS, BEAMS), BEAMS)
            for j in range(2 * OWN):
                beams[pol, j, line, :] = value[j * BEAMS : (j + 1) * BEAMS, :]
            return carry

        lax.fori_loop(0, FRAMES, steer, 0)

        @pl.when(half == 0)
        def _():
            beams[pol, :, : HISTORY * BEAMS, :] = jnp.zeros((2 * OWN, HISTORY * BEAMS, FINE), F32)
            halo_copy(pol).start()

        @pl.when(half == 1)
        def _():
            halo_copy(pol).wait_recv()

        def filter_station(station, carry):
            for part in range(2):
                for tile in range(NT):
                    lanes = slice(tile * LANES, (tile + 1) * LANES)
                    taps = [
                        jnp.broadcast_to(taps_ref[j : j + 1, lanes], (BEAMS, LANES))
                        for j in range(TAPS)
                    ]
                    outs = []
                    for frame in range(FRAMES):
                        total = None
                        for j in range(TAPS):
                            line = (frame + HISTORY - j) * BEAMS
                            term = taps[j] * beams[
                                pol, part * OWN + station, line : line + BEAMS, lanes
                            ]
                            total = term if total is None else total + term
                        outs.append(total)
                        if frame % 2:
                            base = pl.multiple_of(
                                station * FRAMES * BEAMS + (frame - 1) * BEAMS, 2 * BEAMS
                            )
                            lane = part * FINE + tile * LANES
                            filtered[pl.ds(base, 2 * BEAMS), lane : lane + LANES] = (
                                jnp.concatenate(outs, axis=0).astype(BF16)
                            )
                            outs = []
            return carry

        lax.fori_loop(0, OWN, filter_station, 0)

        def transform(station, carry):
            lines = pl.ds(pl.multiple_of(station * FRAMES * BEAMS, FRAMES * BEAMS), FRAMES * BEAMS)
            value = jnp.dot(filtered[lines, :], tab_ref[...], preferred_element_type=F32)
            formed[0, pol * OWN + station] = value.astype(BF16)
            squares = jnp.sum((value * value).reshape(FRAMES, BEAMS, 2 * FINE), axis=0)
            squares = sum(squares[:, k * LANES : (k + 1) * LANES] for k in range(4))
            total = jnp.sum(squares, axis=1, keepdims=True)
            power[...] += jnp.where(lane_id == station * POL + pol, total, 0.0)
            return carry

        lax.fori_loop(0, OWN, transform, 0)

        def send_chunk(station, carry):
            for copy in chunk_copies(pol * OWN + station):
                copy.start()
            return carry

        lax.fori_loop(0, OWN, send_chunk, 0)

    def power_copy(step):
        return remote(
            power, power_all.at[step - 1], p_send.at[step - 1], p_recv.at[step - 1],
            chan=lax.rem(chan + step, CHAN),
        )

    for step in range(1, CHAN):
        power_copy(step).start()
    for step in range(1, CHAN):
        power_copy(step).wait_recv()
    total = power[...]
    for step in range(1, CHAN):
        total = total + power_all[step - 1]
    inverse[0] = lax.rsqrt(total / DENOMINATOR + EPSILON)
    inverse_copies = [
        remote(inverse.at[0], inverse.at[slot], i_send.at[slot], i_recv.at[slot], stn=target)
        for slot, target in ((1, down), (2, far), (3, up), (4, pair))
    ]

    def lane_of(slot, index):
        tile = inverse[slot]
        one = jnp.sum(jnp.where(lane_id == index, tile, 0.0), axis=1, keepdims=True)
        return jnp.broadcast_to(one, (BEAMS, LANES))

    def scale_chunk(which, slot, station):
        for pol in range(POL):
            factor = lane_of(slot, station * POL + pol) * (1.0 / FRAMES)
            for pairs in range(FRAMES // 2):
                lines = slice(pairs * 2 * BEAMS, (pairs + 1) * 2 * BEAMS)
                for tile in range(4):
                    lanes = slice(tile * LANES, (tile + 1) * LANES)
                    value = formed[slot, pol * OWN + station, lines, lanes].astype(F32)
                    scaled[which, station * POL + pol, lines, lanes] = jnp.concatenate(
                        [value[:BEAMS] * factor, value[BEAMS:] * factor], axis=0
                    )

    def correlate(which, slot, station, unit, swapped):
        for q in range(POL):
            factor = lane_of(slot, station * POL + q)
            for tile in range(NT):
                re_lanes = slice(tile * LANES, (tile + 1) * LANES)
                im_lanes = slice(FINE + tile * LANES, FINE + (tile + 1) * LANES)
                real = [None] * (OWN * POL)
                imag = [None] * (OWN * POL)
                for pairs in range(FRAMES // 2):
                    lines = slice(pairs * 2 * BEAMS, (pairs + 1) * 2 * BEAMS)
                    right_re = formed[slot, q * OWN + station, lines, re_lanes].astype(F32)
                    right_im = formed[slot, q * OWN + station, lines, im_lanes].astype(F32)
                    for part in range(2):
                        cr = right_re[part * BEAMS : (part + 1) * BEAMS]
                        ci = right_im[part * BEAMS : (part + 1) * BEAMS]
                        line = (pairs * 2 + part) * BEAMS
                        for c in range(OWN * POL):
                            ar = scaled[which, c, line : line + BEAMS, re_lanes]
                            ai = scaled[which, c, line : line + BEAMS, im_lanes]
                            re = ar * cr + ai * ci
                            im = ar * ci - ai * cr if swapped else ai * cr - ar * ci
                            real[c] = re if real[c] is None else real[c] + re
                            imag[c] = im if imag[c] is None else imag[c] + im
                for c in range(OWN * POL):
                    s, p = c // POL, c % POL
                    line = q * 4 + tile * 2 + p if swapped else p * 4 + tile * 2 + q
                    lines = pl.ds(line, BEAMS, stride=8)
                    stage[0, s, lines, :] = real[c] * factor
                    stage[1, s, lines, :] = imag[c] * factor
        packed[unit] = stage[...].astype(BF16)

    def out_copy(unit, block, station):
        return pltpu.make_async_copy(
            packed.at[unit], out_ref.at[:, :, block * OWN + station], o_sem.at[unit]
        )

    def arrived(slot, chunk):
        remote(
            formed.at[slot, chunk], formed.at[slot, chunk], g_send.at[0, chunk],
            g_recv.at[slot, chunk], stn=up,
        ).wait_recv()

    def forward_up(station):
        return remote(
            formed.at[3, station], formed.at[2, station],
            f_send.at[0, station], g_recv.at[2, station], stn=up,
        )

    def forward_down(station):
        chunk = OWN + station
        return remote(
            formed.at[1, chunk], formed.at[2, chunk],
            f_send.at[1, station], g_recv.at[2, chunk], stn=down,
        )

    for copy in inverse_copies:
        copy.start()

    def own_scale(station, carry):
        scale_chunk(0, 0, station)
        return carry

    lax.fori_loop(0, OWN, own_scale, 0)

    def pass_on(station, carry):
        arrived(3, station)
        forward_up(station).start()
        arrived(1, station)
        arrived(4, station)
        return carry

    def own_pairs(station, carry):
        pass_on(station, carry)
        correlate(0, 0, station, station, False)
        out_copy(station, me, station).start()
        return carry

    lax.fori_loop(0, OWN, own_pairs, 0)
    for copy in inverse_copies:
        copy.wait_recv()

    def near_pairs(station, carry):
        chunk = OWN + station
        arrived(1, chunk)
        forward_down(station).start()
        arrived(3, chunk)
        arrived(4, chunk)
        scale_chunk(1, 4, station)
        for n, slot in enumerate((1, 3, 4)):
            unit = OWN * (1 + n) + station
            correlate(0, slot, station, unit, False)
            out_copy(unit, peers[slot], station).start()
        return carry

    lax.fori_loop(0, OWN, near_pairs, 0)

    theirs = pl.ds(pl.multiple_of(pair * OWN, OWN), OWN)

    def swap_copy(n, station):
        return remote(
            packed.at[5 * OWN + n * OWN + station], out_ref.at[:, station, theirs],
            x_send.at[n, station], x_recv.at[n, station], stn=(up, down)[n],
        )

    def far_copy(station):
        return remote(
            packed.at[7 * OWN + station], out_ref.at[:, :, far * OWN + station],
            x_send.at[2, station], x_recv.at[2, station], stn=pair,
        )

    def swapped_pairs(station, carry):
        for n, slot in enumerate((1, 3)):
            correlate(1, slot, station, 5 * OWN + n * OWN + station, True)
            swap_copy(n, station).start()
        return carry

    lax.fori_loop(0, OWN, swapped_pairs, 0)

    def far_pairs(station, carry):
        arrived(2, station)
        arrived(2, OWN + station)
        correlate(1, 2, station, 7 * OWN + station, False)
        far_copy(station).start()
        correlate(0, 2, station, 4 * OWN + station, False)
        out_copy(4 * OWN + station, far, station).start()
        return carry

    lax.fori_loop(0, OWN, far_pairs, 0)

    def finish(station, carry):
        for n in range(2):
            swap_copy(n, station).wait()
        far_copy(station).wait()
        forward_up(station).wait_send()
        forward_down(station).wait_send()
        out_copy(station, me, station).wait()
        for n, slot in enumerate((1, 3, 4)):
            out_copy(OWN * (1 + n) + station, peers[slot], station).wait()
        out_copy(4 * OWN + station, far, station).wait()
        for pol in range(POL):
            for copy in chunk_copies(pol * OWN + station):
                copy.wait_send()
        return carry

    lax.fori_loop(0, OWN, finish, 0)

    def finish_sends(step, carry):
        dish_copy(0, step).wait_send()
        dish_copy(1, step).wait_send()
        weight_copy(step).wait_send()
        power_copy(step).wait_send()
        return carry

    lax.fori_loop(1, STN, finish_sends, 0)
    for copy in inverse_copies:
        copy.wait_send()

    @pl.when(half == 0)
    def _():
        for pol in range(POL):
            halo_copy(pol).wait_send()


def dish_order(station_map, beam_index, weight_table):
    dishes = station_map.shape[0]
    index = jnp.arange(dishes, dtype=jnp.int32)
    holder = station_map // OWN
    same = (holder[:, None] == holder[None, :]) & (index[None, :] < index[:, None])
    slot = holder * SHARE + jnp.sum(same.astype(jnp.int32), axis=1)
    hot = slot[None, :] == index[:, None]
    perm = jnp.sum(jnp.where(hot, index[None, :], 0), axis=1)
    station = jnp.sum(jnp.where(hot, (station_map % OWN)[None, :], 0), axis=1)
    table_row = jnp.sum(jnp.where(hot, beam_index[None, :], 0), axis=1)
    weight_re, weight_im = weight_table[0, :, 0, :], weight_table[1, :, 0, :]
    table = jnp.stack(
        [jnp.stack([weight_re, weight_im]), jnp.stack([-weight_im, weight_re])]
    )
    rows = table.shape[2]
    row_hot = table_row[:, None] == jnp.arange(rows, dtype=jnp.int32)[None, :]
    chosen = jnp.sum(
        jnp.where(row_hot[:, None, None, :, None], table[None].astype(F32), 0.0), axis=3
    )
    own_hot = station[:, None] == jnp.arange(OWN, dtype=jnp.int32)[None, :]
    steer = jnp.where(own_hot[:, None, None, :, None], chosen[:, :, :, None, :], 0.0)
    steer = steer.reshape(STN, SHARE, 2, 2 * OWN * BEAMS).swapaxes(1, 2)
    steer = steer.reshape(STN, 2 * SHARE, 2 * OWN * BEAMS)
    steer = jnp.pad(steer, ((0, 0), (0, 0), (0, LANES - 2 * OWN * BEAMS)))
    return perm.astype(jnp.int32), steer.astype(BF16)


def per_device(voltages, fir_taps, station_map, beam_index, weight_table):
    perm, steer = dish_order(station_map, beam_index, weight_table)
    parts, _, dishes, frames, pols, fine = voltages.shape
    rows = voltages.reshape(parts, dishes, frames, pols, NT, LANES)
    rows = rows.swapaxes(3, 4).reshape(parts, dishes, frames * NT * pols, LANES)
    table = jnp.asarray(dft_table(), BF16)
    vmem = pl.BlockSpec(memory_space=pltpu.VMEM)
    dma = pltpu.SemaphoreType.DMA
    chunk = (FRAMES * BEAMS, 2 * FINE)
    units = 8 * OWN
    result = pl.pallas_call(
        kernel,
        out_shape=jax.ShapeDtypeStruct((2, OWN, STN * OWN, 8 * BEAMS, LANES), BF16),
        in_specs=[pl.BlockSpec(memory_space=pltpu.SMEM)] + [vmem] * 4,
        out_specs=pl.BlockSpec(memory_space=pl.ANY),
        scratch_shapes=[
            pltpu.VMEM((2 * SHARE * PITCH, LANES), F32),
            pltpu.VMEM((STN - 1, POL, 2 * SHARE, FRAMES * FINE), BF16),
            pltpu.VMEM((POL, STN * 2 * SHARE, FRAMES * FINE), BF16),
            pltpu.VMEM((STN * 2 * SHARE, LANES), BF16),
            pltpu.VMEM((2 * OWN * BEAMS, STN * 2 * SHARE), BF16),
            pltpu.VMEM((POL, 2 * OWN, (HISTORY + FRAMES) * BEAMS, FINE), F32),
            pltpu.VMEM((OWN * FRAMES * BEAMS, 2 * FINE), BF16),
            pltpu.VMEM((5, POL * OWN, *chunk), BF16),
            pltpu.VMEM((2, OWN * POL, *chunk), F32),
            pltpu.VMEM((2, OWN, 8 * BEAMS, LANES), F32),
            pltpu.VMEM((units, 2, OWN, 8 * BEAMS, LANES), BF16),
            pltpu.VMEM((BEAMS, LANES), F32),
            pltpu.VMEM((CHAN - 1, BEAMS, LANES), F32),
            pltpu.VMEM((5, BEAMS, LANES), F32),
            dma((POL, STN - 1)), dma((POL, STN - 1)),
            dma((STN - 1,)), dma((STN - 1,)),
            dma((POL,)), dma((POL,)),
            dma((3, POL * OWN)), dma((5, POL * OWN)), dma((2, OWN)),
            dma((CHAN - 1,)), dma((CHAN - 1,)),
            dma((5,)), dma((5,)),
            dma((5 * OWN,)),
            dma((3, OWN)), dma((3, OWN)),
        ],
        compiler_params=pltpu.CompilerParams(
            collective_id=0, has_side_effects=True, vmem_limit_bytes=48 * 1024 * 1024
        ),
    )(perm, rows, steer, fir_taps, table)
    result = result.reshape(2, OWN, STN * OWN, BEAMS, POL, NT, POL, LANES)
    result = result.swapaxes(5, 6).reshape(2, 1, OWN, STN * OWN, BEAMS, POL, POL, fine)
    return result.astype(F32)[None]


def solution(mesh):
    in_specs = (
        P(None, "chan", "stn", "tm", None, None),
        P(),
        P("stn"),
        P("stn"),
        P(None, None, "chan", None),
    )
    out_specs = P("tm", None, "chan", "stn", None, None, None, None, None)
    return jax.shard_map(
        per_device, mesh=mesh, in_specs=in_specs, out_specs=out_specs, check_vma=False
    )
```

time: 419 us -> 104 us (0.25)
  local copies, waits for them, and re-layouts: 125 us -> 4.69 us
  waiting for transfers between devices: 115 us -> 0 us
  Pallas kernels: 0 us -> 89.4 us
  matrix products: 81.3 us -> 0 us
  blocking collectives: 34.8 us -> 0 us
  other arithmetic: 35.2 us -> 9.23 us
  between operations: 13.7 us -> 0.1 us
  starting transfers between devices: 13.1 us -> 0 us
    all_gather x1 -> x0, waiting for transfers between devices: 103 us -> none  [per_device(): lax.all_gather(normed, 'stn', axis=0, tiled=True)]
    pallas_call x0 -> x1, Pallas kernels: none -> 89.4 us  [per_device(): pl.pallas_call(kernel, out_shape=jax.ShapeDtypeStruct((2, OWN, STN * OWN,...]
    dot_general x10 -> x0, matrix products: 81.2 us -> none  [the longest x4 67.4 us: product(): jnp.einsum('sbcfpk,tbcfqk->cstbpqk', first_part, second_part, preferred_e...]
    unnamed x21 -> x6, local copies, waits for them, and re-layouts: 60.1 us -> 3.34 us
    another operation x15 -> x1, local copies, waits for them, and re-layouts: 38.8 us -> 0.7 us  [dish_order(): jnp.stack([weight_re, weight_im])]
    convert_element_type x5 -> x1, other arithmetic: 28.1 us -> 0.01 us  [dish_order(): table[None].astype(F32)]
    all_gather x1 -> x0, blocking collectives: 25.7 us -> none  [rows_first(): whole = lax.all_gather(both, axis, axis=0, tiled=True)]
    slice x5 -> x0, local copies, waits for them, and re-layouts: 13.6 us -> none  [the longest x1 6.3 us: correlate(): right_re = right_beams[:, 0]]
  transfers between devices with their start and end apart: 4 -> 0, of which waited for: 3 -> 0; matrix products, arithmetic and copies ran while one was open for 3% -> 0% of each run, Pallas kernels for 0% -> 0%
where the time goes in v1:
time: 104 us; the launch traced here: 103 us
  Pallas kernels  89.4 us (86%)
  other arithmetic  9.23 us (9%)
  local copies, waits for them, and re-layouts  4.69 us (5%)
    pallas_call x1, Pallas kernels, per_device(): pl.pallas_call(kernel, out_shape=jax.ShapeDtypeStruct((2, OWN, STN * OWN,...  89.4 us
    unnamed x1, other arithmetic  6.64 us
    unnamed x6, local copies, waits for them, and re-layouts  3.34 us

profile of v1, /device:TPU:1, one launch (start us, length us, event | category | flops | bytes accessed | tf_op | source)
XLA Modules:
  0.0 103.5 jit_solution(1872889622406151228)
XLA Ops:
  0.0 0.7 and_select_fusion.1
  0.7 0.2 convert_reduce_fusion
  0.9 0.8 select_reduce_fusion.2
  1.7 0.7 fusion.2
  2.4 0.7 slice_bitcast_fusion
  3.1 0.1 copy.15
  3.2 0.1 select_reduce_fusion
  3.4 0.1 broadcast_in_dim.89
  3.5 0.2 broadcast_in_dim.96
  3.7 0.1 fusion
  3.8 0.2 copy.16
  4.0 0.0 copy-start
  4.0 1.6 %copy-done = bf16[2,1,64,16,2,256]{5,4,3,2,1,0:T(2,128)(2,1)S(1)} copy-done((bf16[2,1,64,16,2,256]{5,4,3,2,1,0:T(2,128)(2,1)S(1)}, bf16[2,1,64,16,2,256]{5,4,3,2,1,0:T(2,128)(2,1)}, u32[]{:S(2)}) %copy-start) | copy-done | bytes 2097176
  5.6 0.0 copy-start.1
  5.6 1.0 %copy-done.1 = bf16[512,512]{1,0:T(8,128)(2,1)S(1)} copy-done((bf16[512,512]{1,0:T(8,128)(2,1)S(1)}, bf16[512,512]{1,0:T(8,128)(2,1)}, u32[]{:S(2)}) %copy-start.1) | copy-done | bytes 524312
  6.6 0.0 copy-start.2
  6.7 0.7 copy-done.2
  7.4 89.4 %shard_map.64 = bf16[2,4,32,64,128]{4,3,2,1,0:T(8,128)(2,1)} custom-call(s32[64]{0:T(128)S(1)} %get-tuple-element.7.perm_ref, bf16[2,64,64,128]{3,2,1,0:T(8,128)(2,1)S(1)} %bitcast.34, bf16[8,16,128]{2,1,0:T(8,128)(2,1)S(1)} %pad.5.wt_ref, f32[16,256]{1,0:T(8,128)S(1)} %copy-done.2, bf16[512,512]{1,0:T(8,128)(2,1)S(1)} %copy-done.1), custom_call_target="tpu_custom_call" | custom-call | tf_op jit(solution)/shard_map/pallas_call | solution.py:454
  96.8 6.6 %convert.16 = f32[2,4,32,64,128]{4,3,2,1,0:T(8,128)} convert(bf16[2,4,32,64,128]{4,3,2,1,0:T(8,128)(2,1)} %shard_map.64) | non-fusion elementwise | flops 2097152 | bytes 12582912
  (8 shorter events, 0.1 us)
Async XLA Ops:
  4.0 1.6 %copy-start = (bf16[2,1,64,16,2,256]{5,4,3,2,1,0:T(2,128)(2,1)S(1)}, bf16[2,1,64,16,2,256]{5,4,3,2,1,0:T(2,128)(2,1)}, u32[]{:S(2)}) copy-start(bf16[2,1,64,16,2,256]{5,4,3,2,1,0:T(2,128)(2,1)} %param.6) | copy-start | bytes 6291460
  5.6 1.0 %copy-start.1 = (bf16[512,512]{1,0:T(8,128)(2,1)S(1)}, bf16[512,512]{1,0:T(8,128)(2,1)}, u32[]{:S(2)}) copy-start(bf16[512,512]{1,0:T(8,128)(2,1)} %constant.38.clone.tab_ref) | copy-start | bytes 1572868
  6.6 0.7 copy-start.2

commit v2 on v1

--- a/solution.py
+++ b/solution.py
@@ -17,6 +17,7 @@
 CHAN = 8
 SHARE = 8
 OWN = 4
+HALF = OWN // 2
 BEAMS = 8
 POL = 2
 FRAMES = 16
@@ -25,8 +26,14 @@
 LANES = 128
 NT = FINE // LANES
 HISTORY = TAPS - 1
+VMEM_GRANT = 67043328 - 4 * 1024 * 1024
 PITCH = 72
 DENOMINATOR = float(CHAN * FRAMES * FINE)
+
+
+WIDEN_STEPS = 16
+WIDEN_GRANT = 62 * 1024 * 1024
+ROUTE = ((1, 0), (0, 1), (0, 3), (1, 1), (1, 3), (0, 2), (1, 2))
 
 
 def dft_table():
@@ -37,11 +44,11 @@
 
 
 def kernel(
-    perm_ref, v_ref, wt_ref, taps_ref, tab_ref, out_ref,
-    regroup, send_v, recv_v, recv_wt, weights, beams, filtered, formed, scaled, stage, packed,
+    perm_ref, map_hbm, row_hbm, table_hbm, v_hbm, taps_hbm, tab_hbm, out_ref,
+    map_ref, row_ref, table_ref, v_ref, taps_ref, tab_ref, wt_ref, regroup, send_v, recv_v, recv_wt, weights, beams, filtered, formed, scaled, stage, packed, land_swap, land_far,
     power, power_all, inverse,
     a_send, a_recv, w_send, w_recv, h_send, h_recv, g_send, g_recv, f_send,
-    p_send, p_recv, i_send, i_recv, o_sem, x_send, x_recv,
+    p_send, p_recv, i_send, i_recv, o_sem, x_send, x_recv, y_send, y_recv, load_sem,
 ):
     half = lax.axis_index("tm")
     me = lax.axis_index("stn")
@@ -51,7 +58,7 @@
     down = row * RING + lax.rem(col + 3, RING)
     far = row * RING + lax.rem(col + 2, RING)
     pair = (1 - row) * RING + col
-    peers = {1: up, 2: far, 3: down, 4: pair}
+    peers = {0: me, 1: up, 2: far, 3: down, 4: pair}
 
     def remote(src, dst, send, recv, **where):
         return pltpu.make_async_remote_copy(
@@ -70,8 +77,61 @@
             barrier, inc=1, device_id={"chan": lax.rem(chan + step, CHAN)}, device_id_type=MESH
         )
 
-    def regrouped(step, store):
-        holder = lax.rem(me + step, STN)
+    loads = [
+        pltpu.make_async_copy(source, target, load_sem.at[k])
+        for k, (source, target) in enumerate(
+            (
+                (map_hbm, map_ref), (row_hbm, row_ref), (table_hbm, table_ref),
+                (v_hbm, v_ref), (taps_hbm, taps_ref), (tab_hbm, tab_ref),
+            )
+        )
+    ]
+    for load in loads:
+        load.start()
+    loads[0].wait()
+    loads[1].wait()
+
+    dishes = STN * SHARE
+    line_id = lax.broadcasted_iota(jnp.int32, (dishes, dishes), 0)
+    column_id = lax.broadcasted_iota(jnp.int32, (dishes, dishes), 1)
+
+    def over_lanes(mask, value):
+        return jnp.sum(jnp.where(mask, value, 0).astype(F32), axis=1, keepdims=True)
+
+    def over_lines(mask, value):
+        return jnp.sum(jnp.where(mask, value, 0).astype(F32), axis=0, keepdims=True)
+
+    station_all = jnp.broadcast_to(map_ref[...], (dishes, dishes))
+    row_all = jnp.broadcast_to(row_ref[...], (dishes, dishes))
+    holder_across = station_all // OWN
+    holder_line = over_lanes(line_id == column_id, holder_across).astype(jnp.int32)
+    holder_down = jnp.broadcast_to(holder_line, (dishes, dishes))
+    same = holder_across == holder_down
+    rank_across = over_lines(same & (line_id < column_id), 1).astype(jnp.int32)
+    hot = holder_across * SHARE + rank_across == line_id
+    station_slot = over_lanes(hot, station_all % OWN).astype(jnp.int32)
+    row_slot = over_lanes(hot, row_all).astype(jnp.int32)
+
+    loads[2].wait()
+    rows = table_ref.shape[2]
+    weight_re, weight_im = table_ref[0].astype(F32), table_ref[1].astype(F32)
+    blank = jnp.zeros((LANES - 2 * OWN * BEAMS, rows), F32)
+    row_hot = (row_slot == lax.broadcasted_iota(jnp.int32, (dishes, rows), 1)).astype(F32)
+    lane_station = lax.broadcasted_iota(jnp.int32, (dishes, LANES), 1) // BEAMS % OWN
+    chosen = []
+    for first, second in ((weight_re, weight_im), (-weight_im, weight_re)):
+        spread = jnp.concatenate([first] * OWN + [second] * OWN + [blank], axis=0)
+        value = lax.dot_general(
+            row_hot.astype(BF16), spread.astype(BF16), (((1,), (1,)), ((), ())),
+            preferred_element_type=F32,
+        )
+        chosen.append(jnp.where(lane_station == station_slot, value, 0.0))
+    for holder in range(STN):
+        lines = slice(holder * SHARE, (holder + 1) * SHARE)
+        wt_ref[holder] = jnp.concatenate([part[lines] for part in chosen], axis=0).astype(BF16)
+    loads[3].wait()
+
+    def regrouped(holder, store):
         for part in range(2):
             for e in range(SHARE):
                 dish = perm_ref[holder * SHARE + e]
@@ -84,47 +144,51 @@
 
     mine = pl.ds(pl.multiple_of(me * 2 * SHARE, 2 * SHARE), 2 * SHARE)
 
+    def holder_at(step):
+        rows_away, ring_away = ROUTE[step]
+        return (1 - row if rows_away else row) * RING + lax.rem(col + ring_away, RING)
+
     def dish_copy(pol, step):
         return remote(
-            send_v.at[step - 1, pol], recv_v.at[pol, mine],
-            a_send.at[pol, step - 1], a_recv.at[pol, step - 1], stn=lax.rem(me + step, STN),
+            send_v.at[step, pol], recv_v.at[pol, mine],
+            a_send.at[pol, step], a_recv.at[pol, step], stn=holder_at(step),
         )
 
     def weight_copy(step):
-        holder = lax.rem(me + step, STN)
-        return remote(
-            wt_ref.at[holder], recv_wt.at[mine], w_send.at[step - 1], w_recv.at[step - 1], stn=holder
-        )
-
-    def prepare(step, carry):
+        holder = holder_at(step)
+        return remote(
+            wt_ref.at[holder], recv_wt.at[mine], w_send.at[step], w_recv.at[step], stn=holder
+        )
+
+    def prepare(step):
         def store(pol, lane, value):
-            send_v[step - 1, pol, :, lane : lane + LANES] = value
-
-        regrouped(step, store)
-        return carry
-
-    def prepare_and_send(step, carry):
-        prepare(step, carry)
-        dish_copy(0, step - 1).start()
-        return carry
-
-    prepare(1, 0)
+            send_v[step, pol, :, lane : lane + LANES] = value
+
+        regrouped(holder_at(step), store)
+
+    steps = range(STN - 1)
+    prepare(0)
+    prepare(1)
     pl.semaphore_wait(barrier, 1 + (STN - 1) + (CHAN - 1))
-    for step in range(1, STN):
-        weight_copy(step).start()
-    lax.fori_loop(2, STN, prepare_and_send, 0)
+    for step in steps:
+        if step >= 2:
+            prepare(step)
+        if step >= 1:
+            dish_copy(0, step - 1).start()
 
     def store_own(pol, lane, value):
         recv_v[pol, mine, lane : lane + LANES] = value
 
-    regrouped(0, store_own)
-    dish_copy(0, STN - 1).start()
-    lax.fori_loop(1, STN, lambda step, c: (dish_copy(1, step).start(), c)[1], 0)
+    regrouped(me, store_own)
+    dish_copy(0, STN - 2).start()
+    for step in steps:
+        weight_copy(step).start()
+        dish_copy(1, step).start()
     recv_wt[mine, :] = wt_ref[me]
     power[...] = jnp.zeros_like(power)
     lane_id = lax.broadcasted_iota(jnp.int32, (BEAMS, LANES), 1)
 
-    for step in range(1, STN):
+    for step in steps:
         weight_copy(step).wait_recv()
     weights[...] = jnp.transpose(recv_wt[...].astype(F32))[: 2 * OWN * BEAMS, :].astype(BF16)
 
@@ -135,16 +199,26 @@
             h_send.at[pol], h_recv.at[pol], tm=1 - half,
         )
 
-    def chunk_copies(chunk):
-        own = formed.at[0, chunk]
-        return (
-            remote(own, formed.at[3, chunk], g_send.at[0, chunk], g_recv.at[3, chunk], stn=up),
-            remote(own, formed.at[1, chunk], g_send.at[1, chunk], g_recv.at[1, chunk], stn=down),
-            remote(own, formed.at[4, chunk], g_send.at[2, chunk], g_recv.at[4, chunk], stn=pair),
-        )
+    def chunk_copy(chunk, way):
+        slot, target = ((3, up), (1, down), (4, pair))[way]
+        return remote(
+            formed.at[0, chunk], formed.at[slot, chunk],
+            g_send.at[way, chunk], g_recv.at[slot, chunk], stn=target,
+        )
+
+    loads[4].wait()
+    loads[5].wait()
+    UP, DOWN, PAIR = range(3)
+
+    def send_first(station, carry):
+        chunk_copy(station, UP).start()
+        chunk_copy(lax.rem(station + HALF, OWN), DOWN).start()
+        chunk_copy(station, PAIR).start()
+        return carry
 
     for pol in range(POL):
-        lax.fori_loop(1, STN, lambda step, c: (dish_copy(pol, step).wait_recv(), c)[1], 0)
+        for step in steps:
+            dish_copy(pol, step).wait_recv()
 
         def steer(frame, carry):
             lanes = pl.ds(pl.multiple_of(frame * FINE, FINE), FINE)
@@ -208,12 +282,28 @@
 
         lax.fori_loop(0, OWN, transform, 0)
 
-        def send_chunk(station, carry):
-            for copy in chunk_copies(pol * OWN + station):
-                copy.start()
-            return carry
-
-        lax.fori_loop(0, OWN, send_chunk, 0)
+        if pol == 0:
+            lax.fori_loop(0, OWN, send_first, 0)
+
+    def arrived(slot, chunk):
+        remote(
+            formed.at[slot, chunk], formed.at[slot, chunk], g_send.at[0, chunk],
+            g_recv.at[slot, chunk], stn=up,
+        ).wait_recv()
+
+    def forward_up(pol, n):
+        chunk = pol * OWN + n
+        return remote(
+            formed.at[3, chunk], formed.at[2, chunk],
+            f_send.at[0, pol, n], g_recv.at[2, chunk], stn=up,
+        )
+
+    def forward_down(pol, n):
+        chunk = pol * OWN + HALF + n
+        return remote(
+            formed.at[1, chunk], formed.at[2, chunk],
+            f_send.at[1, pol, n], g_recv.at[2, chunk], stn=down,
+        )
 
     def power_copy(step):
         return remote(
@@ -223,6 +313,19 @@
 
     for step in range(1, CHAN):
         power_copy(step).start()
+
+    def send_second(n, carry):
+        chunk_copy(OWN + n, UP).start()
+        chunk_copy(OWN + HALF + n, DOWN).start()
+        chunk_copy(OWN + 2 * n, PAIR).start()
+        chunk_copy(OWN + 2 * n + 1, PAIR).start()
+        arrived(3, n)
+        forward_up(0, n).start()
+        arrived(1, HALF + n)
+        forward_down(0, n).start()
+        return carry
+
+    lax.fori_loop(0, HALF, send_second, 0)
     for step in range(1, CHAN):
         power_copy(step).wait_recv()
     total = power[...]
@@ -251,7 +354,7 @@
                         [value[:BEAMS] * factor, value[BEAMS:] * factor], axis=0
                     )
 
-    def correlate(which, slot, station, unit, swapped):
+    def correlate(which, slot, station, swapped):
         for q in range(POL):
             factor = lane_of(slot, station * POL + q)
             for tile in range(NT):
@@ -280,32 +383,12 @@
                     lines = pl.ds(line, BEAMS, stride=8)
                     stage[0, s, lines, :] = real[c] * factor
                     stage[1, s, lines, :] = imag[c] * factor
-        packed[unit] = stage[...].astype(BF16)
 
     def out_copy(unit, block, station):
         return pltpu.make_async_copy(
             packed.at[unit], out_ref.at[:, :, block * OWN + station], o_sem.at[unit]
         )
 
-    def arrived(slot, chunk):
-        remote(
-            formed.at[slot, chunk], formed.at[slot, chunk], g_send.at[0, chunk],
-            g_recv.at[slot, chunk], stn=up,
-        ).wait_recv()
-
-    def forward_up(station):
-        return remote(
-            formed.at[3, station], formed.at[2, station],
-            f_send.at[0, station], g_recv.at[2, station], stn=up,
-        )
-
-    def forward_down(station):
-        chunk = OWN + station
-        return remote(
-            formed.at[1, chunk], formed.at[2, chunk],
-            f_send.at[1, station], g_recv.at[2, chunk], stn=down,
-        )
-
     for copy in inverse_copies:
         copy.start()
 
@@ -315,16 +398,9 @@
 
     lax.fori_loop(0, OWN, own_scale, 0)
 
-    def pass_on(station, carry):
-        arrived(3, station)
-        forward_up(station).start()
-        arrived(1, station)
-        arrived(4, station)
-        return carry
-
     def own_pairs(station, carry):
-        pass_on(station, carry)
-        correlate(0, 0, station, station, False)
+        correlate(0, 0, station, False)
+        packed[station] = stage[...].astype(BF16)
         out_copy(station, me, station).start()
         return carry
 
@@ -332,79 +408,150 @@
     for copy in inverse_copies:
         copy.wait_recv()
 
-    def near_pairs(station, carry):
-        chunk = OWN + station
-        arrived(1, chunk)
-        forward_down(station).start()
-        arrived(3, chunk)
-        arrived(4, chunk)
-        scale_chunk(1, 4, station)
-        for n, slot in enumerate((1, 3, 4)):
-            unit = OWN * (1 + n) + station
-            correlate(0, slot, station, unit, False)
-            out_copy(unit, peers[slot], station).start()
-        return carry
-
-    lax.fori_loop(0, OWN, near_pairs, 0)
-
-    theirs = pl.ds(pl.multiple_of(pair * OWN, OWN), OWN)
+    def neighbour_pairs(n, station):
+        slot = 3 - 2 * n
+        unit = slot * OWN + station
+        correlate(0, slot, station, False)
+        packed[unit] = stage[...].astype(BF16)
+        out_copy(unit, row * RING + lax.rem(col + slot, RING), station).start()
+
+    def first_pairs(k, carry):
+        arrived(3, OWN + k)
+        forward_up(1, k).start()
+        arrived(1, OWN + HALF + k)
+        forward_down(1, k).start()
+        chunk_copy(OWN + HALF + k, UP).start()
+        chunk_copy(OWN + k, DOWN).start()
+
+        def near(n, c):
+            neighbour_pairs(n, k + HALF * n)
+            return c
+
+        lax.fori_loop(0, 2, near, 0)
+
+        def partner(n, c):
+            station = 2 * k + n
+            arrived(4, station)
+            arrived(4, OWN + station)
+            scale_chunk(1, 4, station)
+            unit = 4 * OWN + station
+            correlate(0, 4, station, False)
+            packed[unit] = stage[...].astype(BF16)
+            out_copy(unit, pair, station).start()
+            return c
+
+        lax.fori_loop(0, 2, partner, 0)
+        return carry
+
+    lax.fori_loop(0, HALF, first_pairs, 0)
+
+    across = [(1 - row) * RING + lax.rem(col + step, RING) for step in range(RING)]
 
     def swap_copy(n, station):
         return remote(
-            packed.at[5 * OWN + n * OWN + station], out_ref.at[:, station, theirs],
-            x_send.at[n, station], x_recv.at[n, station], stn=(up, down)[n],
+            packed.at[5 * OWN + n * OWN + station], land_swap.at[n, station],
+            x_send.at[n, station], x_recv.at[n, station],
+            stn=row * RING + lax.rem(col + 3 - 2 * n, RING),
         )
 
     def far_copy(station):
         return remote(
-            packed.at[7 * OWN + station], out_ref.at[:, :, far * OWN + station],
-            x_send.at[2, station], x_recv.at[2, station], stn=pair,
-        )
-
-    def swapped_pairs(station, carry):
-        for n, slot in enumerate((1, 3)):
-            correlate(1, slot, station, 5 * OWN + n * OWN + station, True)
-            swap_copy(n, station).start()
-        return carry
-
-    lax.fori_loop(0, OWN, swapped_pairs, 0)
-
-    def far_pairs(station, carry):
+            packed.at[7 * OWN + station], land_far.at[station],
+            y_send.at[station], y_recv.at[station], stn=pair,
+        )
+
+    def swap_out(n, station):
+        block = (1 - row) * RING + lax.rem(col + 1 + 2 * n, RING)
+        stations = pl.ds(pl.multiple_of(block * OWN, OWN), OWN)
+        return pltpu.make_async_copy(
+            land_swap.at[n, station], out_ref.at[:, station, stations], x_recv.at[n, station]
+        )
+
+    def far_out(station):
+        return pltpu.make_async_copy(
+            land_far.at[station], out_ref.at[:, :, across[2] * OWN + station], y_recv.at[station]
+        )
+
+    def swapped_pairs(n, station):
+        correlate(1, 3 - 2 * n, station, True)
+        packed[5 * OWN + n * OWN + station] = stage[...].astype(BF16)
+        swap_copy(n, station).start()
+
+    def first_swaps(k, carry):
+        n = lax.rem(k, 2)
+        swapped_pairs(n, k // 2 + HALF * n)
+        return carry
+
+    def far_pairs(k, carry):
+        station = lax.rem(k, 2) * HALF + k // 2
         arrived(2, station)
         arrived(2, OWN + station)
-        correlate(1, 2, station, 7 * OWN + station, False)
+        correlate(1, 2, station, False)
+        packed[7 * OWN + station] = stage[...].astype(BF16)
         far_copy(station).start()
-        correlate(0, 2, station, 4 * OWN + station, False)
-        out_copy(4 * OWN + station, far, station).start()
-        return carry
-
+        return carry
+
+    def last_pairs(k, carry):
+        n = lax.rem(k, 2)
+        station = lax.rem(HALF + k // 2 + HALF * n, OWN)
+        slot = 3 - 2 * n
+        arrived(slot, station)
+        arrived(slot, OWN + station)
+        swapped_pairs(n, station)
+        neighbour_pairs(n, station)
+        return carry
+
+    def far_own_pairs(station, carry):
+        unit = 2 * OWN + station
+        correlate(0, 2, station, False)
+        packed[unit] = stage[...].astype(BF16)
+        out_copy(unit, far, station).start()
+        return carry
+
+    lax.fori_loop(0, 2 * HALF, first_swaps, 0)
     lax.fori_loop(0, OWN, far_pairs, 0)
+    lax.fori_loop(0, 2 * HALF, last_pairs, 0)
+    lax.fori_loop(0, OWN, far_own_pairs, 0)
+
+    def land_far_pairs(station, carry):
+        far_copy(station).wait_recv()
+        far_out(station).start()
+        return carry
+
+    def land_swaps(k, carry):
+        n = lax.rem(k, 2)
+        station = lax.rem(k // 2 + HALF * n, OWN)
+        swap_copy(n, station).wait_recv()
+        swap_out(n, station).start()
+        return carry
+
+    lax.fori_loop(0, OWN, land_far_pairs, 0)
+    lax.fori_loop(0, 2 * OWN, land_swaps, 0)
 
     def finish(station, carry):
         for n in range(2):
-            swap_copy(n, station).wait()
-        far_copy(station).wait()
-        forward_up(station).wait_send()
-        forward_down(station).wait_send()
-        out_copy(station, me, station).wait()
-        for n, slot in enumerate((1, 3, 4)):
-            out_copy(OWN * (1 + n) + station, peers[slot], station).wait()
-        out_copy(4 * OWN + station, far, station).wait()
+            swap_copy(n, station).wait_send()
+            swap_out(n, station).wait()
+        far_copy(station).wait_send()
+        far_out(station).wait()
+        for slot in range(5):
+            out_copy(slot * OWN + station, peers[slot], station).wait()
         for pol in range(POL):
-            for copy in chunk_copies(pol * OWN + station):
-                copy.wait_send()
+            for way in (UP, DOWN, PAIR):
+                chunk_copy(pol * OWN + station, way).wait_send()
         return carry
 
     lax.fori_loop(0, OWN, finish, 0)
-
-    def finish_sends(step, carry):
+    for pol in range(POL):
+        for n in range(HALF):
+            forward_up(pol, n).wait_send()
+            forward_down(pol, n).wait_send()
+    for step in steps:
         dish_copy(0, step).wait_send()
         dish_copy(1, step).wait_send()
         weight_copy(step).wait_send()
+    for step in range(1, CHAN):
         power_copy(step).wait_send()
-        return carry
-
-    lax.fori_loop(1, STN, finish_sends, 0)
     for copy in inverse_copies:
         copy.wait_send()
 
@@ -414,49 +561,73 @@
             halo_copy(pol).wait_send()
 
 
-def dish_order(station_map, beam_index, weight_table):
-    dishes = station_map.shape[0]
-    index = jnp.arange(dishes, dtype=jnp.int32)
+def widen(narrow_hbm, wide_hbm, narrow, wide, in_sem, out_sem):
+    size = narrow.shape[0] // WIDEN_STEPS
+    pieces = [pl.ds(step * size, size) for step in range(WIDEN_STEPS)]
+    loads = [
+        pltpu.make_async_copy(narrow_hbm.at[piece], narrow.at[piece], in_sem.at[step])
+        for step, piece in enumerate(pieces)
+    ]
+    stores = [
+        pltpu.make_async_copy(wide.at[piece], wide_hbm.at[piece], out_sem.at[step])
+        for step, piece in enumerate(pieces)
+    ]
+    for load in loads:
+        load.start()
+    for piece, load, store in zip(pieces, loads, stores):
+        load.wait()
+        wide[piece] = narrow[piece].astype(F32)
+        store.start()
+    for store in stores:
+        store.wait()
+
+
+def widened(array):
+    shape = array.shape
+    flat = array.reshape(-1, LANES)
+    hbm = pl.BlockSpec(memory_space=pltpu.HBM)
+    wide = pl.pallas_call(
+        widen,
+        out_shape=jax.ShapeDtypeStruct(flat.shape, F32),
+        in_specs=[hbm],
+        out_specs=hbm,
+        scratch_shapes=[
+            pltpu.VMEM(flat.shape, BF16), pltpu.VMEM(flat.shape, F32),
+            pltpu.SemaphoreType.DMA((WIDEN_STEPS,)), pltpu.SemaphoreType.DMA((WIDEN_STEPS,)),
+        ],
+        compiler_params=pltpu.CompilerParams(vmem_limit_bytes=WIDEN_GRANT),
+    )(flat)
+    return wide.reshape(shape)
+
+
+def dish_order(station_map):
+    index = jnp.arange(station_map.shape[0], dtype=jnp.int32)
     holder = station_map // OWN
-    same = (holder[:, None] == holder[None, :]) & (index[None, :] < index[:, None])
-    slot = holder * SHARE + jnp.sum(same.astype(jnp.int32), axis=1)
-    hot = slot[None, :] == index[:, None]
-    perm = jnp.sum(jnp.where(hot, index[None, :], 0), axis=1)
-    station = jnp.sum(jnp.where(hot, (station_map % OWN)[None, :], 0), axis=1)
-    table_row = jnp.sum(jnp.where(hot, beam_index[None, :], 0), axis=1)
-    weight_re, weight_im = weight_table[0, :, 0, :], weight_table[1, :, 0, :]
-    table = jnp.stack(
-        [jnp.stack([weight_re, weight_im]), jnp.stack([-weight_im, weight_re])]
-    )
-    rows = table.shape[2]
-    row_hot = table_row[:, None] == jnp.arange(rows, dtype=jnp.int32)[None, :]
-    chosen = jnp.sum(
-        jnp.where(row_hot[:, None, None, :, None], table[None].astype(F32), 0.0), axis=3
-    )
-    own_hot = station[:, None] == jnp.arange(OWN, dtype=jnp.int32)[None, :]
-    steer = jnp.where(own_hot[:, None, None, :, None], chosen[:, :, :, None, :], 0.0)
-    steer = steer.reshape(STN, SHARE, 2, 2 * OWN * BEAMS).swapaxes(1, 2)
-    steer = steer.reshape(STN, 2 * SHARE, 2 * OWN * BEAMS)
-    steer = jnp.pad(steer, ((0, 0), (0, 0), (0, LANES - 2 * OWN * BEAMS)))
-    return perm.astype(jnp.int32), steer.astype(BF16)
+    earlier = (holder[:, None] == holder[None, :]) & (index[None, :] < index[:, None])
+    slot = holder * SHARE + jnp.sum(earlier.astype(jnp.int32), axis=1)
+    return jnp.sum(jnp.where(slot[None, :] == index[:, None], index[None, :], 0), axis=1)
 
 
 def per_device(voltages, fir_taps, station_map, beam_index, weight_table):
-    perm, steer = dish_order(station_map, beam_index, weight_table)
     parts, _, dishes, frames, pols, fine = voltages.shape
     rows = voltages.reshape(parts, dishes, frames, pols, NT, LANES)
     rows = rows.swapaxes(3, 4).reshape(parts, dishes, frames * NT * pols, LANES)
     table = jnp.asarray(dft_table(), BF16)
-    vmem = pl.BlockSpec(memory_space=pltpu.VMEM)
+    weights = jnp.transpose(weight_table[:, :, 0, :], (0, 2, 1))
+    hbm = pl.BlockSpec(memory_space=pltpu.HBM)
     dma = pltpu.SemaphoreType.DMA
     chunk = (FRAMES * BEAMS, 2 * FINE)
-    units = 8 * OWN
+    operands = (
+        station_map[None], beam_index[None], weights, rows, fir_taps, table,
+    )
     result = pl.pallas_call(
         kernel,
         out_shape=jax.ShapeDtypeStruct((2, OWN, STN * OWN, 8 * BEAMS, LANES), BF16),
-        in_specs=[pl.BlockSpec(memory_space=pltpu.SMEM)] + [vmem] * 4,
-        out_specs=pl.BlockSpec(memory_space=pl.ANY),
+        in_specs=[pl.BlockSpec(memory_space=pltpu.SMEM)] + [hbm] * len(operands),
+        out_specs=hbm,
         scratch_shapes=[
+            *(pltpu.VMEM(a.shape, a.dtype) for a in operands),
+            pltpu.VMEM((STN, 2 * SHARE, LANES), BF16),
             pltpu.VMEM((2 * SHARE * PITCH, LANES), F32),
             pltpu.VMEM((STN - 1, POL, 2 * SHARE, FRAMES * FINE), BF16),
             pltpu.VMEM((POL, STN * 2 * SHARE, FRAMES * FINE), BF16),
@@ -467,26 +638,30 @@
             pltpu.VMEM((5, POL * OWN, *chunk), BF16),
             pltpu.VMEM((2, OWN * POL, *chunk), F32),
             pltpu.VMEM((2, OWN, 8 * BEAMS, LANES), F32),
-            pltpu.VMEM((units, 2, OWN, 8 * BEAMS, LANES), BF16),
+            pltpu.VMEM((8 * OWN, 2, OWN, 8 * BEAMS, LANES), BF16),
+            pltpu.VMEM((2, OWN, 2, OWN, 8 * BEAMS, LANES), BF16),
+            pltpu.VMEM((OWN, 2, OWN, 8 * BEAMS, LANES), BF16),
             pltpu.VMEM((BEAMS, LANES), F32),
             pltpu.VMEM((CHAN - 1, BEAMS, LANES), F32),
             pltpu.VMEM((5, BEAMS, LANES), F32),
             dma((POL, STN - 1)), dma((POL, STN - 1)),
             dma((STN - 1,)), dma((STN - 1,)),
             dma((POL,)), dma((POL,)),
-            dma((3, POL * OWN)), dma((5, POL * OWN)), dma((2, OWN)),
+            dma((3, POL * OWN)), dma((5, POL * OWN)), dma((2, POL, HALF)),
             dma((CHAN - 1,)), dma((CHAN - 1,)),
             dma((5,)), dma((5,)),
             dma((5 * OWN,)),
-            dma((3, OWN)), dma((3, OWN)),
+            dma((2, OWN)), dma((2, OWN)),
+            dma((OWN,)), dma((OWN,)),
+            dma((len(operands),)),
         ],
         compiler_params=pltpu.CompilerParams(
-            collective_id=0, has_side_effects=True, vmem_limit_bytes=48 * 1024 * 1024
+            collective_id=0, has_side_effects=True, vmem_limit_bytes=VMEM_GRANT
         ),
-    )(perm, rows, steer, fir_taps, table)
-    result = result.reshape(2, OWN, STN * OWN, BEAMS, POL, NT, POL, LANES)
+    )(dish_order(station_map), *operands)
+    result = widened(result).reshape(2, OWN, STN * OWN, BEAMS, POL, NT, POL, LANES)
     result = result.swapaxes(5, 6).reshape(2, 1, OWN, STN * OWN, BEAMS, POL, POL, fine)
-    return result.astype(F32)[None]
+    return result[None]
 
 
 def solution(mesh):

time: 104 us -> 97.8 us (0.940)
  other arithmetic: 9.23 us -> 2.14 us
  Pallas kernels: 89.4 us -> 95.5 us
  local copies, waits for them, and re-layouts: 4.69 us -> 0 us
    unnamed x1 -> x0, other arithmetic: 6.64 us -> none
    pallas_call x0 -> x1, Pallas kernels: none -> 4.54 us  [widened(): pl.pallas_call(widen, out_shape=jax.ShapeDtypeStruct(flat.shape, F32), in...]
    unnamed x6 -> x0, local copies, waits for them, and re-layouts: 3.34 us -> none
    pallas_call x1, Pallas kernels: 89.4 us -> 90.9 us  [per_device(): pl.pallas_call(kernel, out_shape=jax.ShapeDtypeStruct((2, OWN, STN * OWN,...]
where the time goes in v2:
time: 97.8 us; the launch traced here: 97.6 us
  Pallas kernels  95.5 us (98%)
  other arithmetic  2.14 us (2%)
    pallas_call x1, Pallas kernels, per_device(): pl.pallas_call(kernel, out_shape=jax.ShapeDtypeStruct((2, OWN, STN * OWN,...  90.9 us
    pallas_call x1, Pallas kernels, widened(): pl.pallas_call(widen, out_shape=jax.ShapeDtypeStruct(flat.shape, F32), in...  4.54 us

profile of v2, /device:TPU:1, one launch (start us, length us, event | category | flops | bytes accessed | tf_op | source)
XLA Modules:
  0.0 97.6 jit_solution(5224528820780894129)
XLA Ops:
  0.0 0.7 and_select_fusion
  0.7 0.2 convert_reduce_fusion
  0.8 0.7 multiply_add_fusion
  1.5 0.6 select_reduce_fusion.perm_ref
  2.1 90.9 %shard_map.64 = bf16[2,4,32,64,128]{4,3,2,1,0:T(8,128)(2,1)} custom-call(s32[64]{0:T(128)} %select_reduce_fusion.perm_ref, s32[1,64]{1,0:T(1,128)} %bitcast.19, s32[1,64]{1,0:T(1,128)} %bitcast.20, bf16[2,8,16]{2,1,0:T(8,128)(2,1)} %bitcast.18, bf16[2,64,64,128]{3,2,1,0:T(8,128)(2,1)} %bitcast.17, f32[16,256]{1,0:T(8,128)} %taps_hbm.1, ...), custom_call_target="tpu_custom_call" | custom-call | tf_op jit(solution)/shard_map/pallas_call | solution.py:623
  93.1 4.5 %shard_map.65 = f32[16384,128]{1,0:T(8,128)} custom-call(bf16[16384,128]{1,0:T(8,128)(2,1)} %bitcast.16), custom_call_target="tpu_custom_call" | custom-call | tf_op jit(solution)/shard_map/pallas_call | solution.py:589

commit v3 on v2

--- a/solution.py
+++ b/solution.py
@@ -33,7 +33,7 @@
 
 WIDEN_STEPS = 16
 WIDEN_GRANT = 62 * 1024 * 1024
-ROUTE = ((1, 0), (0, 1), (0, 3), (1, 1), (1, 3), (0, 2), (1, 2))
+ROUTE = ((1, 2), (1, 1), (1, 3), (1, 0), (0, 2), (0, 1), (0, 3))
 
 
 def dft_table():
@@ -44,11 +44,11 @@
 
 
 def kernel(
-    perm_ref, map_hbm, row_hbm, table_hbm, v_hbm, taps_hbm, tab_hbm, out_ref,
-    map_ref, row_ref, table_ref, v_ref, taps_ref, tab_ref, wt_ref, regroup, send_v, recv_v, recv_wt, weights, beams, filtered, formed, scaled, stage, packed, land_swap, land_far,
+    map_hbm, row_hbm, table_hbm, v_hbm, taps_hbm, tab_hbm, out_ref,
+    map_ref, row_ref, table_ref, v_ref, taps_ref, tab_ref, perm_vec, perm_ref, wt_ref, regroup, send_v, recv_v, recv_wt, weights, beams, filtered, formed, scaled, stage, packed, land_swap, land_far,
     power, power_all, inverse,
     a_send, a_recv, w_send, w_recv, h_send, h_recv, g_send, g_recv, f_send,
-    p_send, p_recv, i_send, i_recv, o_sem, x_send, x_recv, y_send, y_recv, load_sem,
+    p_send, p_recv, i_send, i_recv, o_sem, x_send, x_recv, y_send, y_recv, load_sem, perm_sem,
 ):
     half = lax.axis_index("tm")
     me = lax.axis_index("stn")
@@ -96,21 +96,26 @@
     column_id = lax.broadcasted_iota(jnp.int32, (dishes, dishes), 1)
 
     def over_lanes(mask, value):
-        return jnp.sum(jnp.where(mask, value, 0).astype(F32), axis=1, keepdims=True)
+        return jnp.sum(jnp.where(mask, value, 0), axis=1, keepdims=True, dtype=jnp.int32)
 
     def over_lines(mask, value):
-        return jnp.sum(jnp.where(mask, value, 0).astype(F32), axis=0, keepdims=True)
+        return jnp.sum(jnp.where(mask, value, 0), axis=0, keepdims=True, dtype=jnp.int32)
 
     station_all = jnp.broadcast_to(map_ref[...], (dishes, dishes))
     row_all = jnp.broadcast_to(row_ref[...], (dishes, dishes))
     holder_across = station_all // OWN
-    holder_line = over_lanes(line_id == column_id, holder_across).astype(jnp.int32)
+    holder_line = over_lanes(line_id == column_id, holder_across)
     holder_down = jnp.broadcast_to(holder_line, (dishes, dishes))
     same = holder_across == holder_down
-    rank_across = over_lines(same & (line_id < column_id), 1).astype(jnp.int32)
+    rank_down = over_lanes(same & (column_id < line_id), 1)
+    slot_down = holder_down * SHARE + rank_down
+    perm_vec[...] = over_lines(slot_down == column_id, line_id)
+    perm_copy = pltpu.make_async_copy(perm_vec, perm_ref, perm_sem)
+    perm_copy.start()
+    rank_across = over_lines(same & (line_id < column_id), 1)
     hot = holder_across * SHARE + rank_across == line_id
-    station_slot = over_lanes(hot, station_all % OWN).astype(jnp.int32)
-    row_slot = over_lanes(hot, row_all).astype(jnp.int32)
+    station_slot = over_lanes(hot, station_all % OWN)
+    row_slot = over_lanes(hot, row_all)
 
     loads[2].wait()
     rows = table_ref.shape[2]
@@ -130,11 +135,12 @@
         lines = slice(holder * SHARE, (holder + 1) * SHARE)
         wt_ref[holder] = jnp.concatenate([part[lines] for part in chosen], axis=0).astype(BF16)
     loads[3].wait()
+    perm_copy.wait()
 
     def regrouped(holder, store):
         for part in range(2):
             for e in range(SHARE):
-                dish = perm_ref[holder * SHARE + e]
+                dish = perm_ref[0, holder * SHARE + e]
                 line = (part * SHARE + e) * PITCH
                 regroup[line : line + FRAMES * NT * POL, :] = v_ref[part, dish].astype(F32)
         for pol in range(POL):
@@ -600,14 +606,6 @@
     return wide.reshape(shape)
 
 
-def dish_order(station_map):
-    index = jnp.arange(station_map.shape[0], dtype=jnp.int32)
-    holder = station_map // OWN
-    earlier = (holder[:, None] == holder[None, :]) & (index[None, :] < index[:, None])
-    slot = holder * SHARE + jnp.sum(earlier.astype(jnp.int32), axis=1)
-    return jnp.sum(jnp.where(slot[None, :] == index[:, None], index[None, :], 0), axis=1)
-
-
 def per_device(voltages, fir_taps, station_map, beam_index, weight_table):
     parts, _, dishes, frames, pols, fine = voltages.shape
     rows = voltages.reshape(parts, dishes, frames, pols, NT, LANES)
@@ -623,10 +621,12 @@
     result = pl.pallas_call(
         kernel,
         out_shape=jax.ShapeDtypeStruct((2, OWN, STN * OWN, 8 * BEAMS, LANES), BF16),
-        in_specs=[pl.BlockSpec(memory_space=pltpu.SMEM)] + [hbm] * len(operands),
+        in_specs=[hbm] * len(operands),
         out_specs=hbm,
         scratch_shapes=[
             *(pltpu.VMEM(a.shape, a.dtype) for a in operands),
+            pltpu.VMEM((1, dishes), jnp.int32),
+            pltpu.SMEM((1, dishes), jnp.int32),
             pltpu.VMEM((STN, 2 * SHARE, LANES), BF16),
             pltpu.VMEM((2 * SHARE * PITCH, LANES), F32),
             pltpu.VMEM((STN - 1, POL, 2 * SHARE, FRAMES * FINE), BF16),
@@ -653,12 +653,12 @@
             dma((5 * OWN,)),
             dma((2, OWN)), dma((2, OWN)),
             dma((OWN,)), dma((OWN,)),
-            dma((len(operands),)),
+            dma((len(operands),)), dma,
         ],
         compiler_params=pltpu.CompilerParams(
             collective_id=0, has_side_effects=True, vmem_limit_bytes=VMEM_GRANT
         ),
-    )(dish_order(station_map), *operands)
+    )(*operands)
     result = widened(result).reshape(2, OWN, STN * OWN, BEAMS, POL, NT, POL, LANES)
     result = result.swapaxes(5, 6).reshape(2, 1, OWN, STN * OWN, BEAMS, POL, POL, fine)
     return result[None]

time: 97.8 us -> 92.7 us (0.948)
  Pallas kernels: 95.5 us -> 92.6 us
  other arithmetic: 2.14 us -> 0 us
    pallas_call x1, Pallas kernels: 90.9 us -> 88 us  [per_device(): pl.pallas_call(kernel, out_shape=jax.ShapeDtypeStruct((2, OWN, STN * OWN,...]
where the time goes in v3:
time: 92.7 us; the launch traced here: 92.6 us
  Pallas kernels  92.6 us (100%)
    pallas_call x1, Pallas kernels, per_device(): pl.pallas_call(kernel, out_shape=jax.ShapeDtypeStruct((2, OWN, STN * OWN,...  88 us
    pallas_call x1, Pallas kernels, widened(): pl.pallas_call(widen, out_shape=jax.ShapeDtypeStruct(flat.shape, F32), in...  4.54 us

profile of v3, /device:TPU:1, one launch (start us, length us, event | category | flops | bytes accessed | tf_op | source)
XLA Modules:
  0.0 92.6 jit_solution(1898059515370934238)
XLA Ops:
  0.0 88.0 %shard_map.64 = bf16[2,4,32,64,128]{4,3,2,1,0:T(8,128)(2,1)} custom-call(s32[1,64]{1,0:T(1,128)} %bitcast.19, s32[1,64]{1,0:T(1,128)} %bitcast.20, bf16[2,8,16]{2,1,0:T(8,128)(2,1)} %bitcast.18, bf16[2,64,64,128]{3,2,1,0:T(8,128)(2,1)} %bitcast.17, f32[16,256]{1,0:T(8,128)} %taps_hbm.1, bf16[512,512]{1,0:T(8,128)(2,1)} %constant.2.clone.tab_hbm), custom_call_target="tpu_custom_call" | custom-call | tf_op jit(solution)/shard_map/pallas_call | solution.py:621
  88.0 4.5 %shard_map.65 = f32[16384,128]{1,0:T(8,128)} custom-call(bf16[16384,128]{1,0:T(8,128)(2,1)} %bitcast.16), custom_call_target="tpu_custom_call" | custom-call | tf_op jit(solution)/shard_map/pallas_call | solution.py:595

commit v4 on v3

--- a/solution.py
+++ b/solution.py
@@ -34,6 +34,7 @@
 WIDEN_STEPS = 16
 WIDEN_GRANT = 62 * 1024 * 1024
 ROUTE = ((1, 2), (1, 1), (1, 3), (1, 0), (0, 2), (0, 1), (0, 3))
+SECOND = (3, 2, 1, 0, 6, 5, 4)
 
 
 def dft_table():
@@ -189,6 +190,7 @@
     dish_copy(0, STN - 2).start()
     for step in steps:
         weight_copy(step).start()
+    for step in SECOND:
         dish_copy(1, step).start()
     recv_wt[mine, :] = wt_ref[me]
     power[...] = jnp.zeros_like(power)

time: 92.7 us -> 88 us (0.949)
  Pallas kernels: 92.6 us -> 87.9 us
    pallas_call x1, Pallas kernels: 88 us -> 83.3 us  [per_device(): pl.pallas_call(kernel, out_shape=jax.ShapeDtypeStruct((2, OWN, STN * OWN,...]
where the time goes in v4:
time: 88 us; the launch traced here: 87.9 us
  Pallas kernels  87.9 us (100%)
    pallas_call x1, Pallas kernels, per_device(): pl.pallas_call(kernel, out_shape=jax.ShapeDtypeStruct((2, OWN, STN * OWN,...  83.3 us
    pallas_call x1, Pallas kernels, widened(): pl.pallas_call(widen, out_shape=jax.ShapeDtypeStruct(flat.shape, F32), in...  4.54 us

profile of v4, /device:TPU:1, one launch (start us, length us, event | category | flops | bytes accessed | tf_op | source)
XLA Modules:
  0.0 87.9 jit_solution(18119644158025886749)
XLA Ops:
  0.0 83.3 %shard_map.64 = bf16[2,4,32,64,128]{4,3,2,1,0:T(8,128)(2,1)} custom-call(s32[1,64]{1,0:T(1,128)} %bitcast.19, s32[1,64]{1,0:T(1,128)} %bitcast.20, bf16[2,8,16]{2,1,0:T(8,128)(2,1)} %bitcast.18, bf16[2,64,64,128]{3,2,1,0:T(8,128)(2,1)} %bitcast.17, f32[16,256]{1,0:T(8,128)} %taps_hbm.1, bf16[512,512]{1,0:T(8,128)(2,1)} %constant.2.clone.tab_hbm), custom_call_target="tpu_custom_call" | custom-call | tf_op jit(solution)/shard_map/pallas_call | solution.py:623
  83.3 4.5 %shard_map.65 = f32[16384,128]{1,0:T(8,128)} custom-call(bf16[16384,128]{1,0:T(8,128)(2,1)} %bitcast.16), custom_call_target="tpu_custom_call" | custom-call | tf_op jit(solution)/shard_map/pallas_call | solution.py:597
